TPU v7x, 32 devices: a whole 2x2x4 slice. The times are simulated.
32 devices in a mesh: row: 4 (over z), col: 8 (over y, x, core).
Axes of the slice: x: 2, y: 2, z: 4, core: 2. Of those that a mesh axis runs over, the one named last changes fastest.
Arguments:
- a_matrix: float32 [8192, 8192], P('row', 'col'), may hold values from -14 to 30, as said below
- b_matrix: float32 [4096, 4096], P('row', 'col'), may hold values from -14 to 30, as said below
- c_matrix: float32 [8192, 4096], P('row', 'col'), may hold values from -6 to 6
Outputs:
- a_swept: float32 [8192, 8192], P('row', 'col')
- c_swept: float32 [8192, 4096], P('row', 'col')
- b_next: float32 [4096, 4096], P('row', 'col')
Inputs may be any that keep to these rules, and one draw needn't show every extreme that they name: `a_matrix`: symmetric positive definite; its smallest eigenvalue is at least 1. `b_matrix`: symmetric positive definite; its smallest eigenvalue is at least 1.
All inputs are finite; a program needn't handle non-finite values. Where the computation divides by a largest or mean magnitude, that divisor is 1e-20 or more.
Results may differ from a plain program's by a relative error of at most 0.00012.
Values sent between devices are 32-bit elements; how exact they have to be, the bound alone decides.
No kernel may reach another device: no remote copies, remote signals or barrier semaphores. Data moves between devices by JAX's collectives and lax.ppermute only.
A program may use at most 128 MiB of HBM per device.

v0:
```python
import jax
import jax.numpy as jnp
from jax import lax
from jax.sharding import PartitionSpec as P

PANEL = 256
PIVOT_ITERS = 6
STEPS_A = 2
STEPS_B = 16
EXACT = lax.Precision.HIGHEST
CLOSE = lax.Precision.HIGH


def spread(value, axis, source):
    kept = jnp.where(lax.axis_index(axis) == source, value, 0).astype(value.dtype)
    return lax.psum(kept, axis)


def pivot_inverse(pivot):
    order = pivot.shape[0]
    unit_square = jnp.eye(order, dtype=jnp.float32)
    scaling = 1.0 / jnp.sqrt(jnp.sum(pivot * unit_square, axis=1))
    unit = pivot * scaling[:, None] * scaling[None, :]
    ceiling = jnp.max(jnp.sum(jnp.abs(unit), axis=1))
    approx = jnp.eye(order, dtype=jnp.float32) / ceiling
    for turn in range(PIVOT_ITERS):
        product = jnp.dot(unit, approx, precision=EXACT, preferred_element_type=jnp.float32)
        approx = 2.0 * approx - jnp.dot(
            approx, product, precision=EXACT, preferred_element_type=jnp.float32
        )
    return approx * scaling[:, None] * scaling[None, :]


def mul(left, right, dims, precision):
    return lax.dot_general(
        left, right, (dims, ((), ())), precision=precision, preferred_element_type=jnp.float32
    )


def sweep_panel(block, panel, places):
    order = block.shape[0]
    index = jnp.arange(order, dtype=jnp.int32)
    eye = (index[:, None] == jnp.concatenate([index, places])[None, :]).astype(jnp.float32)
    both = jnp.concatenate([block, panel], 1)
    for start in range(0, order, PANEL):
        stop = start + PANEL
        inverse = pivot_inverse(both[start:stop, start:stop].T)
        solved = mul(inverse, both[start:stop] - eye[start:stop], ((0,), (0,)), EXACT)
        updated = both - mul(both[:, start:stop], solved, ((1,), (0,)), CLOSE)
        both = jnp.concatenate([updated[:start], eye[start:stop] - solved, updated[stop:]], 0)
    return (both[:, order:], eye[:, order:])


def a_sweep(matrix, other):
    local_rows, local_cols = matrix.shape
    other_cols = other.shape[1]
    order = STEPS_A * PANEL
    row_place = lax.axis_index("row")
    col_place = lax.axis_index("col")
    panel = spread(matrix[:, :order], "col", 0)
    joined = spread(jnp.concatenate([matrix[:order], other[:order], panel[:order]], 1), "row", 0)
    rows = joined[:, : local_cols + other_cols]
    block = joined[:, local_cols + other_cols :].T
    places = row_place * local_rows + jnp.arange(local_rows, dtype=jnp.int32)
    swept, eye = sweep_panel(block, panel.T, places)
    solved = eye - swept
    new_matrix = matrix - mul(solved, rows[:, :local_cols], ((0,), (0,)), CLOSE)
    new_other = other - mul(solved, rows[:, local_cols:], ((0,), (0,)), CLOSE)
    front = jnp.where(col_place == 0, swept.T, new_matrix[:, :order])
    return (new_matrix.at[:, :order].set(front), new_other)


def b_sweep(matrix, row_count, col_count):
    local_rows, local_cols = matrix.shape
    order = min(local_rows, local_cols)
    steps = STEPS_B * PANEL // order
    row_part = order // row_count
    col_part = order // col_count
    row_place = lax.axis_index("row")
    col_place = lax.axis_index("col")
    dealt = matrix.T.reshape(local_cols // order, col_count, col_part, local_rows)
    dealt = lax.all_to_all(dealt, "col", 1, 0, tiled=True).reshape(local_cols, local_rows)
    dealt = dealt.T.reshape(local_rows // order, row_count, row_part, local_cols)
    dealt = lax.all_to_all(dealt, "row", 1, 0, tiled=True).reshape(local_rows, local_cols)
    index = jnp.arange(local_rows, dtype=jnp.int32)
    for step in range(steps):
        top = step * row_part
        left = step * col_part
        panel = lax.all_gather(dealt[:, left : left + col_part].T, "col", axis=0, tiled=True)
        joined = jnp.concatenate([dealt[top : top + row_part], panel[:, top : top + row_part].T], 1)
        joined = lax.all_gather(joined, "row", axis=0, tiled=True)
        rows = joined[:, :local_cols]
        block = joined[:, local_cols:].T
        inside = (index >= top) & (index < top + row_part)
        places = jnp.where(inside, index - top + row_place * row_part, -1)
        swept, eye = sweep_panel(block, panel, places)
        updated = dealt + mul(swept - eye, rows, ((0,), (0,)), CLOSE)
        own = lax.dynamic_slice_in_dim(swept, col_place * col_part, col_part, 0).T
        dealt = updated.at[:, left : left + col_part].set(own)
    back = dealt.reshape(steps, 1, row_part, local_cols)
    back = lax.all_to_all(back, "row", 0, 1, tiled=True).reshape(local_rows, local_cols)
    back = back.T.reshape(steps, 1, col_part, local_rows)
    back = lax.all_to_all(back, "col", 0, 1, tiled=True).reshape(local_cols, local_rows)
    return back.T


def solution(mesh):
    row_count = mesh.shape["row"]
    col_count = mesh.shape["col"]

    def body(a_matrix, b_matrix, c_matrix):
        b_local = jnp.sum(b_matrix * b_matrix)
        a_swept, c_swept = a_sweep(a_matrix, c_matrix)
        b_inverse = b_sweep(b_matrix, row_count, col_count)
        inv_local = jnp.sum(b_inverse * b_inverse)
        sums = lax.psum(jnp.stack([b_local, inv_local]), ("row", "col"))
        scale = jnp.sqrt(jnp.sqrt(sums[1] / sums[0]))
        b_next = 0.5 * (scale * b_matrix + b_inverse / scale)
        return (a_swept, c_swept, b_next)

    return jax.shard_map(
        body,
        mesh=mesh,
        in_specs=(P("row", "col"), P("row", "col"), P("row", "col")),
        out_specs=(P("row", "col"), P("row", "col"), P("row", "col")),
        check_vma=False,
    )
```

profile of v0, /device:TPU:10, one launch (start us, length us, event | category | flops | bytes accessed | tf_op | source)
XLA Modules:
  0.0 1504.4 jit_solution(638320156755108339)
XLA Ops:
  9.2 29.3 %all_to_all.48 = f32[1,8,64,1024]{3,2,0,1:T(8,128)} all-to-all(f32[1,8,64,1024]{3,2,0,1:T(8,128)S(1)} %bitcast.702), channel_id=1, replica_groups=mesh['row'=4,'col'=8] {'col'}, dimensions={1} | all-to-all | bytes 4194304 | tf_op jit(solution)/shard_map/all_to_all | solution.py:82
  40.6 51.6 %all_to_all.49 = f32[2,4,128,512]{3,2,0,1:T(8,128)S(1)} all-to-all(f32[2,4,128,512]{3,2,0,1:T(8,128)S(1)} %copy.155), channel_id=1, replica_groups=mesh['row'=4,'col'=8] {'row'}, dimensions={1} | all-to-all | bytes 4194304 | tf_op jit(solution)/shard_map/all_to_all | solution.py:84
  93.5 27.3 %all-gather.17.cloned.1.call-done = f32[512,1024]{1,0:T(8,128)} async-done(((f32[64,1024]{1,0:T(8,128)}), f32[512,1024]{1,0:T(8,128)}) %all-gather.17.cloned.1.call-update) | async-done | bytes 2097168 | tf_op jit(solution)/shard_map/all_gather | solution.py:89
  125.3 42.9 %all-gather.19.cloned.1.call-done = f32[512,1024]{1,0:T(8,128)} async-done(((f32[128,1024]{1,0:T(8,128)}), f32[512,1024]{1,0:T(8,128)}) %all-gather.19.cloned.1.call-update) | async-done | bytes 2097168 | tf_op jit(solution)/shard_map/all_gather | solution.py:91
  227.9 27.0 %all-gather.21.cloned.1.call-done = f32[512,1024]{1,0:T(8,128)} async-done(((f32[64,1024]{1,0:T(8,128)}), f32[512,1024]{1,0:T(8,128)}) %all-gather.21.cloned.1.call-update) | async-done | bytes 2097168 | tf_op jit(solution)/shard_map/all_gather | solution.py:89
  258.9 43.4 %all-gather.23.cloned.1.call-done = f32[512,1024]{1,0:T(8,128)} async-done(((f32[128,1024]{1,0:T(8,128)}), f32[512,1024]{1,0:T(8,128)}) %all-gather.23.cloned.1.call-update) | async-done | bytes 2097168 | tf_op jit(solution)/shard_map/all_gather | solution.py:91
  362.1 27.0 %all-gather.25.cloned.1.call-done = f32[512,1024]{1,0:T(8,128)} async-done(((f32[64,1024]{1,0:T(8,128)}), f32[512,1024]{1,0:T(8,128)}) %all-gather.25.cloned.1.call-update) | async-done | bytes 2097168 | tf_op jit(solution)/shard_map/all_gather | solution.py:89
  393.4 43.2 %all-gather.27.cloned.1.call-done = f32[512,1024]{1,0:T(8,128)} async-done(((f32[128,1024]{1,0:T(8,128)}), f32[512,1024]{1,0:T(8,128)}) %all-gather.27.cloned.1.call-update) | async-done | bytes 2097168 | tf_op jit(solution)/shard_map/all_gather | solution.py:91
  495.9 27.0 %all-gather.29.cloned.1.call-done = f32[512,1024]{1,0:T(8,128)} async-done(((f32[64,1024]{1,0:T(8,128)}), f32[512,1024]{1,0:T(8,128)}) %all-gather.29.cloned.1.call-update) | async-done | bytes 2097168 | tf_op jit(solution)/shard_map/all_gather | solution.py:89
  527.0 43.3 %all-gather.31.cloned.1.call-done = f32[512,1024]{1,0:T(8,128)} async-done(((f32[128,1024]{1,0:T(8,128)}), f32[512,1024]{1,0:T(8,128)}) %all-gather.31.cloned.1.call-update) | async-done | bytes 2097168 | tf_op jit(solution)/shard_map/all_gather | solution.py:91
  630.3 27.0 %all-gather.33.cloned.1.call-done = f32[512,1024]{1,0:T(8,128)} async-done(((f32[64,1024]{1,0:T(8,128)}), f32[512,1024]{1,0:T(8,128)}) %all-gather.33.cloned.1.call-update) | async-done | bytes 2097168 | tf_op jit(solution)/shard_map/all_gather | solution.py:89
  661.3 43.4 %all-gather.35.cloned.1.call-done = f32[512,1024]{1,0:T(8,128)} async-done(((f32[128,1024]{1,0:T(8,128)}), f32[512,1024]{1,0:T(8,128)}) %all-gather.35.cloned.1.call-update) | async-done | bytes 2097168 | tf_op jit(solution)/shard_map/all_gather | solution.py:91
  764.1 27.0 %all-gather.37.cloned.1.call-done = f32[512,1024]{1,0:T(8,128)} async-done(((f32[64,1024]{1,0:T(8,128)}), f32[512,1024]{1,0:T(8,128)}) %all-gather.37.cloned.1.call-update) | async-done | bytes 2097168 | tf_op jit(solution)/shard_map/all_gather | solution.py:89
  795.3 43.2 %all-gather.39.cloned.1.call-done = f32[512,1024]{1,0:T(8,128)} async-done(((f32[128,1024]{1,0:T(8,128)}), f32[512,1024]{1,0:T(8,128)}) %all-gather.39.cloned.1.call-update) | async-done | bytes 2097168 | tf_op jit(solution)/shard_map/all_gather | solution.py:91
  897.3 4.7 slice_select_fusion
  903.0 22.2 %all-gather.41.cloned.1.call-done = f32[512,1024]{1,0:T(8,128)} async-done(((f32[64,1024]{1,0:T(8,128)}), f32[512,1024]{1,0:T(8,128)}) %all-gather.41.cloned.1.call-update) | async-done | bytes 2097168 | tf_op jit(solution)/shard_map/all_gather | solution.py:89
  936.7 73.2 %all-reduce.3.cloned.1.call-done = f32[2048,512]{1,0:T(8,128)} async-done(((f32[2048,512]{1,0:T(8,128)}), f32[2048,512]{1,0:T(8,128)}) %all-reduce.3.cloned.1.call-update) | async-done | bytes 4194320 | tf_op jit(solution)/shard_map/psum | solution.py:16
  1015.8 39.9 %all-gather.43.cloned.1.call-done = f32[512,1024]{1,0:T(8,128)} async-done(((f32[128,1024]{1,0:T(8,128)}), f32[512,1024]{1,0:T(8,128)}) %all-gather.43.cloned.1.call-update) | async-done | bytes 2097168 | tf_op jit(solution)/shard_map/all_gather | solution.py:91
  1121.3 90.3 %all-reduce.5.cloned.1.call-done = f32[512,2048]{1,0:T(8,128)} async-done(((f32[512,2048]{1,0:T(8,128)}), f32[512,2048]{1,0:T(8,128)}) %all-reduce.5.cloned.1.call-update) | async-done | bytes 4194320 | tf_op jit(solution)/shard_map/psum | solution.py:16
  1223.5 18.7 %all-gather.45.cloned.1.call-done = f32[512,1024]{1,0:T(8,128)} async-done(((f32[64,1024]{1,0:T(8,128)}), f32[512,1024]{1,0:T(8,128)}) %all-gather.45.cloned.1.call-update) | async-done | bytes 2097168 | tf_op jit(solution)/shard_map/all_gather | solution.py:89
  1251.4 7.1 fusion.13
  1270.0 22.7 %all-gather.47.cloned.1.call-done = f32[512,1024]{1,0:T(8,128)} async-done(((f32[128,1024]{1,0:T(8,128)}), f32[512,1024]{1,0:T(8,128)}) %all-gather.47.cloned.1.call-update) | async-done | bytes 2097168 | tf_op jit(solution)/shard_map/all_gather | solution.py:91
  1348.6 6.7 all-to-all-start.2
  1367.4 7.8 fusion.15
  1378.5 5.6 slice_subtract_fusion.3
  1385.7 4.6 fusion.234
  1390.3 9.9 all-to-all-done.2
  1403.9 5.1 all-to-all-start.3
  1414.6 11.6 convolution_subtract_fusion
  1426.3 5.8 fusion.2
  1438.4 9.8 convolution_subtract_fusion.9
  1448.2 42.8 %psum.23 = f32[2]{0:T(128)S(1)} all-reduce(f32[2]{0:T(128)S(1)} %pad_maximum_fusion.35), channel_id=1, replica_groups=mesh['row'=4,'col'=8] {'row','col'}, use_global_device_ids=true, to_apply=%region_66.67 | all-reduce | flops 2 | bytes 16 | tf_op jit(solution)/shard_map/psum | solution.py:116
  (752 shorter events, 581.9 us)
Async XLA Ops:
  7.2 113.7 %all-gather.17.cloned.1.call-start = ((), (), s32[]{:S(2)}) async-start(), calls=%async_computation.6 | async-start | bytes 2359296 | tf_op jit(solution)/shard_map/all_gather | solution.py:89
  9.1 29.3 %copy-start.55 = (f32[1024,512]{0,1:T(8,128)}, f32[1024,512]{0,1:T(8,128)S(1)}, u32[]{:S(2)}) copy-start(f32[1024,512]{0,1:T(8,128)S(1)} %copy.152) | copy-start | bytes 6291460
  93.3 74.9 %all-gather.19.cloned.1.call-start = ((), (), s32[]{:S(2)}) async-start(), calls=%async_computation.7 | async-start | bytes 2621440 | tf_op jit(solution)/shard_map/all_gather | solution.py:91
  123.7 131.2 %all-gather.21.cloned.1.call-start = ((), (), s32[]{:S(2)}) async-start(), calls=%async_computation.8 | async-start | bytes 2359296 | tf_op jit(solution)/shard_map/all_gather | solution.py:89
  226.9 75.4 %all-gather.23.cloned.1.call-start = ((), (), s32[]{:S(2)}) async-start(), calls=%async_computation.9 | async-start | bytes 2621440 | tf_op jit(solution)/shard_map/all_gather | solution.py:91
  257.8 131.3 %all-gather.25.cloned.1.call-start = ((), (), s32[]{:S(2)}) async-start(), calls=%async_computation.10 | async-start | bytes 2359296 | tf_op jit(solution)/shard_map/all_gather | solution.py:89
  329.4 5.5 copy-start.13
  361.1 75.4 %all-gather.27.cloned.1.call-start = ((), (), s32[]{:S(2)}) async-start(), calls=%async_computation.11 | async-start | bytes 2621440 | tf_op jit(solution)/shard_map/all_gather | solution.py:91
  392.0 130.9 %all-gather.29.cloned.1.call-start = ((), (), s32[]{:S(2)}) async-start(), calls=%async_computation.12 | async-start | bytes 2359296 | tf_op jit(solution)/shard_map/all_gather | solution.py:89
  494.9 75.4 %all-gather.31.cloned.1.call-start = ((), (), s32[]{:S(2)}) async-start(), calls=%async_computation.13 | async-start | bytes 2621440 | tf_op jit(solution)/shard_map/all_gather | solution.py:91
  525.8 131.5 %all-gather.33.cloned.1.call-start = ((), (), s32[]{:S(2)}) async-start(), calls=%async_computation.14 | async-start | bytes 2359296 | tf_op jit(solution)/shard_map/all_gather | solution.py:89
  629.2 75.4 %all-gather.35.cloned.1.call-start = ((), (), s32[]{:S(2)}) async-start(), calls=%async_computation.15 | async-start | bytes 2621440 | tf_op jit(solution)/shard_map/all_gather | solution.py:91
  660.2 130.9 %all-gather.37.cloned.1.call-start = ((), (), s32[]{:S(2)}) async-start(), calls=%async_computation.16 | async-start | bytes 2359296 | tf_op jit(solution)/shard_map/all_gather | solution.py:89
  763.1 75.4 %all-gather.39.cloned.1.call-start = ((), (), s32[]{:S(2)}) async-start(), calls=%async_computation.17 | async-start | bytes 2621440 | tf_op jit(solution)/shard_map/all_gather | solution.py:91
  794.0 131.3 %all-gather.41.cloned.1.call-start = ((), (), s32[]{:S(2)}) async-start(), calls=%async_computation.18 | async-start | bytes 2359296 | tf_op jit(solution)/shard_map/all_gather | solution.py:89
  897.2 112.6 %all-reduce.3.cloned.1.call-start = ((), (), s32[]{:S(2)}) async-start(), calls=%async_computation.4 | async-start | bytes 8388608 | tf_op jit(solution)/shard_map/psum | solution.py:16
  902.0 153.7 %all-gather.43.cloned.1.call-start = ((), (), s32[]{:S(2)}) async-start(), calls=%async_computation.19 | async-start | bytes 2621440 | tf_op jit(solution)/shard_map/all_gather | solution.py:91
  928.1 283.5 %all-reduce.5.cloned.1.call-start = ((), (), s32[]{:S(2)}) async-start(), calls=%async_computation.5 | async-start | bytes 8388608 | tf_op jit(solution)/shard_map/psum | solution.py:16
  928.7 5.8 copy-start.107
  1015.3 226.8 %all-gather.45.cloned.1.call-start = ((), (), s32[]{:S(2)}) async-start(), calls=%async_computation.20 | async-start | bytes 2359296 | tf_op jit(solution)/shard_map/all_gather | solution.py:89
  1117.7 174.9 %all-gather.47.cloned.1.call-start = ((), (), s32[]{:S(2)}) async-start(), calls=%async_computation.21 | async-start | bytes 2621440 | tf_op jit(solution)/shard_map/all_gather | solution.py:91
  1251.4 7.1 copy-start.36
  1348.6 51.7 %all-to-all-start.2 = ((f32[8,1,128,512]{3,2,1,0:T(8,128)}), f32[8,1,128,512]{3,2,1,0:T(8,128)}, u32[]{:S(2)}, u32[]{:S(2)}) async-start(f32[8,1,128,512]{3,2,1,0:T(8,128)} %bitcast.706), calls=%async_computation.2 | async-start | bytes 4194304 | tf_op jit(solution)/shard_map/all_to_all | solution.py:101
  1356.6 10.8 slice-start
  1359.9 7.5 slice-start.1
  1378.5 7.2 copy-start.7
  1378.5 7.2 copy-start.8
  1403.9 8.2 slice-start.2
  1403.9 30.3 %all-to-all-start.3 = ((f32[8,1,64,1024]{3,2,1,0:T(8,128)}), f32[8,1,64,1024]{3,2,1,0:T(8,128)}, u32[]{:S(2)}, u32[]{:S(2)}) async-start(f32[8,1,64,1024]{3,2,1,0:T(8,128)} %bitcast.72), calls=%async_computation.3 | async-start | bytes 4194304 | tf_op jit(solution)/shard_map/all_to_all | solution.py:103
  1409.1 5.5 copy-start.4
  1412.2 14.1 copy-start.3
  1426.3 12.1 copy-start.5
  (101 other events, 236.8 us)
Sparse Core Ops, SparseCore 0:
  93.5 27.2 all-gather.16
  123.8 44.3 all-gather.18
  227.0 27.8 all-gather.20
  257.9 44.3 all-gather.22
  361.2 27.8 all-gather.24
  392.2 44.3 all-gather.26
  495.0 27.8 all-gather.28
  525.9 44.3 all-gather.30
  629.4 27.8 all-gather.32
  660.3 44.3 all-gather.34
  763.2 27.8 all-gather.36
  794.1 44.3 all-gather.38
  897.3 27.8 all-gather.40
  928.9 80.8 all-reduce.2
  1011.2 44.4 all-gather.42
  1058.5 153.1 all-reduce.4
  1213.4 28.6 all-gather.44
  1248.3 44.3 all-gather.46
where the time goes:
time: 1520 us; the launch traced here: 1500 us
  waiting for transfers between devices  701 us (46%)
  matrix products  290 us (19%)
  local copies, waits for them, and re-layouts  229 us (15%)
  blocking collectives  124 us (8%)
  other arithmetic  115 us (8%)
  between operations  31.5 us (2%)
    all_gather x8, waiting for transfers between devices, b_sweep(): joined = lax.all_gather(joined, 'row', axis=0, tiled=True)  322 us
    all_gather x8, waiting for transfers between devices, b_sweep(): lax.all_gather(dealt[:, left:left + col_part].T, 'col', axis=0, tiled=True)  203 us
    psum x2, waiting for transfers between devices, spread(): return lax.psum(kept, axis)  163 us
    dot_general x46, matrix products, mul(): lax.dot_general(left, right, (dims, ((), ())), precision=precision, prefe...  149 us
    dot_general x108, matrix products, pivot_inverse(): jnp.dot(unit, approx, precision=EXACT, preferred_element_type=jnp.float32)  97.6 us
    unnamed x226, local copies, waits for them, and re-layouts  55.5 us
    dot_general x18, local copies, waits for them, and re-layouts, mul(): lax.dot_general(left, right, (dims, ((), ())), precision=precision, prefe...  55.2 us
    all_to_all x1, blocking collectives, b_sweep(): lax.all_to_all(dealt, 'row', 1, 0, tiled=True)  51.6 us
  transfers between devices with their start and end apart: 20, of which 20 were waited for; matrix products, arithmetic and copies ran while one was open for 12% of the time, Pallas kernels for 0%

commit v1 on v0

--- a/solution.py
+++ b/solution.py
@@ -2,6 +2,7 @@
 import jax.numpy as jnp
 from jax import lax
 from jax.sharding import PartitionSpec as P
+from jax.lax import axis_index, ppermute, psum
 
 PANEL = 256
 PIVOT_ITERS = 6
@@ -88,7 +89,20 @@
         left = step * col_part
         panel = lax.all_gather(dealt[:, left : left + col_part].T, "col", axis=0, tiled=True)
         joined = jnp.concatenate([dealt[top : top + row_part], panel[:, top : top + row_part].T], 1)
-        joined = lax.all_gather(joined, "row", axis=0, tiled=True)
+
+        def edge_drive(block_here, link_axis):
+            lanes = psum(1, axis_name=link_axis)
+            value_now = [(dev_i - 1, dev_i) for dev_i in range(1, lanes)] + [(lanes - 1, 0)]
+            mat_out = block_here
+            sides = [mat_out]
+            for _ in range(lanes - 1):
+                mat_out = ppermute(mat_out, axis_name=link_axis, perm=value_now)
+                sides += [mat_out]
+            b_now = jnp.concatenate([*reversed(sides)], 0)
+            finding = axis_index(link_axis)
+            return jnp.roll(b_now, (finding + 1) * mat_out.shape[0], 0)
+
+        joined = edge_drive(joined, "row")
         rows = joined[:, :local_cols]
         block = joined[:, local_cols:].T
         inside = (index >= top) & (index < top + row_part)

time: 1520 us -> 1470 us (0.967)
  waiting for transfers between devices: 701 us -> 609 us
  starting transfers between devices: 13 us -> 44.4 us
  other arithmetic: 115 us -> 136 us
    all_gather x8 -> x0, waiting for transfers between devices: 322 us -> none  [b_sweep(): joined = lax.all_gather(joined, 'row', axis=0, tiled=True)]
    ppermute x0 -> x24, waiting for transfers between devices: none -> 266 us  [edge_drive(): mat_out = ppermute(mat_out, axis_name=link_axis, perm=value_now)]
    ppermute x0 -> x24, starting transfers between devices: none -> 31.5 us  [edge_drive(): mat_out = ppermute(mat_out, axis_name=link_axis, perm=value_now)]
    concatenate x0 -> x8, other arithmetic: none -> 28.6 us  [edge_drive(): return jnp.roll(b_now, (finding + 1) * mat_out.shape[0], 0)]
    psum x2, waiting for transfers between devices: 163 us -> 136 us  [spread(): return lax.psum(kept, axis)]
    unnamed x226 -> x260, local copies, waits for them, and re-layouts: 55.5 us -> 65.1 us
  transfers between devices with their start and end apart: 20 -> 36, of which waited for: 20 -> 35; matrix products, arithmetic and copies ran while one was open for 12% -> 12% of each run, Pallas kernels for 0% -> 0%
where the time goes in v1:
time: 1470 us
  waiting for transfers between devices  609 us (41%)
  matrix products  294 us (20%)
  local copies, waits for them, and re-layouts  228 us (16%)
  other arithmetic  136 us (9%)
  blocking collectives  124 us (8%)
  starting transfers between devices  44.4 us (3%)
  between operations  31 us (2%)
    ppermute x24, waiting for transfers between devices, edge_drive(): mat_out = ppermute(mat_out, axis_name=link_axis, perm=value_now)  266 us
    all_gather x8, waiting for transfers between devices, b_sweep(): lax.all_gather(dealt[:, left:left + col_part].T, 'col', axis=0, tiled=True)  196 us
    dot_general x46, matrix products, mul(): lax.dot_general(left, right, (dims, ((), ())), precision=precision, prefe...  157 us
    psum x2, waiting for transfers between devices, spread(): return lax.psum(kept, axis)  136 us
    dot_general x108, matrix products, pivot_inverse(): jnp.dot(unit, approx, precision=EXACT, preferred_element_type=jnp.float32)  94.2 us
    unnamed x260, local copies, waits for them, and re-layouts  65.1 us
    dot_general x18, local copies, waits for them, and re-layouts, mul(): lax.dot_general(left, right, (dims, ((), ())), precision=precision, prefe...  55.2 us
    all_to_all x1, blocking collectives, b_sweep(): lax.all_to_all(dealt, 'row', 1, 0, tiled=True)  51.6 us
  transfers between devices with their start and end apart: 36, of which 35 were waited for; matrix products, arithmetic and copies ran while one was open for 12% of the time, Pallas kernels for 0%

profile of v1, /device:TPU:10, one launch (start us, length us, event | category | flops | bytes accessed | tf_op | source)
XLA Modules:
  0.0 1465.5 jit_solution(18119118820186917541)
XLA Ops:
  9.2 29.3 %all_to_all.48 = f32[1,8,64,1024]{3,2,0,1:T(8,128)} all-to-all(f32[1,8,64,1024]{3,2,0,1:T(8,128)S(1)} %bitcast.702), channel_id=1, replica_groups=mesh['row'=4,'col'=8] {'col'}, dimensions={1} | all-to-all | bytes 4194304 | tf_op jit(solution)/shard_map/all_to_all | solution.py:83
  40.6 51.6 %all_to_all.49 = f32[2,4,128,512]{3,2,0,1:T(8,128)S(1)} all-to-all(f32[2,4,128,512]{3,2,0,1:T(8,128)S(1)} %copy.155), channel_id=1, replica_groups=mesh['row'=4,'col'=8] {'row'}, dimensions={1} | all-to-all | bytes 4194304 | tf_op jit(solution)/shard_map/all_to_all | solution.py:85
  93.5 27.3 %all-gather.9.cloned.1.call-done = f32[512,1024]{1,0:T(8,128)} async-done(((f32[64,1024]{1,0:T(8,128)}), f32[512,1024]{1,0:T(8,128)}) %all-gather.9.cloned.1.call-update) | async-done | bytes 2097168 | tf_op jit(solution)/shard_map/all_gather | solution.py:90
  124.4 12.6 collective-permute-done
  139.8 11.1 collective-permute-done.1
  152.2 13.2 collective-permute-done.2
  229.3 27.1 %all-gather.11.cloned.1.call-done = f32[512,1024]{1,0:T(8,128)} async-done(((f32[64,1024]{1,0:T(8,128)}), f32[512,1024]{1,0:T(8,128)}) %all-gather.11.cloned.1.call-update) | async-done | bytes 2097168 | tf_op jit(solution)/shard_map/all_gather | solution.py:90
  260.0 12.6 collective-permute-done.3
  275.4 11.0 collective-permute-done.4
  287.6 13.0 collective-permute-done.5
  364.1 27.1 %all-gather.13.cloned.1.call-done = f32[512,1024]{1,0:T(8,128)} async-done(((f32[64,1024]{1,0:T(8,128)}), f32[512,1024]{1,0:T(8,128)}) %all-gather.13.cloned.1.call-update) | async-done | bytes 2097168 | tf_op jit(solution)/shard_map/all_gather | solution.py:90
  394.8 12.6 collective-permute-done.6
  409.5 11.6 collective-permute-done.7
  422.3 13.0 collective-permute-done.8
  498.4 27.1 %all-gather.15.cloned.1.call-done = f32[512,1024]{1,0:T(8,128)} async-done(((f32[64,1024]{1,0:T(8,128)}), f32[512,1024]{1,0:T(8,128)}) %all-gather.15.cloned.1.call-update) | async-done | bytes 2097168 | tf_op jit(solution)/shard_map/all_gather | solution.py:90
  529.0 12.6 collective-permute-done.9
  543.8 11.6 collective-permute-done.10
  556.6 13.0 collective-permute-done.11
  633.0 27.1 %all-gather.17.cloned.1.call-done = f32[512,1024]{1,0:T(8,128)} async-done(((f32[64,1024]{1,0:T(8,128)}), f32[512,1024]{1,0:T(8,128)}) %all-gather.17.cloned.1.call-update) | async-done | bytes 2097168 | tf_op jit(solution)/shard_map/all_gather | solution.py:90
  663.7 12.6 collective-permute-done.12
  678.4 11.6 collective-permute-done.13
  691.2 13.0 collective-permute-done.14
  767.3 27.1 %all-gather.19.cloned.1.call-done = f32[512,1024]{1,0:T(8,128)} async-done(((f32[64,1024]{1,0:T(8,128)}), f32[512,1024]{1,0:T(8,128)}) %all-gather.19.cloned.1.call-update) | async-done | bytes 2097168 | tf_op jit(solution)/shard_map/all_gather | solution.py:90
  798.0 12.6 collective-permute-done.15
  812.7 11.6 collective-permute-done.16
  825.5 13.0 collective-permute-done.17
  906.7 22.3 %all-gather.21.cloned.1.call-done = f32[512,1024]{1,0:T(8,128)} async-done(((f32[64,1024]{1,0:T(8,128)}), f32[512,1024]{1,0:T(8,128)}) %all-gather.21.cloned.1.call-update) | async-done | bytes 2097168 | tf_op jit(solution)/shard_map/all_gather | solution.py:90
  965.3 48.5 %all-reduce.3.cloned.1.call-done = f32[2048,512]{1,0:T(8,128)} async-done(((f32[2048,512]{1,0:T(8,128)}), f32[2048,512]{1,0:T(8,128)}) %all-reduce.3.cloned.1.call-update) | async-done | bytes 4194320 | tf_op jit(solution)/shard_map/psum | solution.py:17
  1085.1 87.5 %all-reduce.5.cloned.1.call-done = f32[512,2048]{1,0:T(8,128)} async-done(((f32[512,2048]{1,0:T(8,128)}), f32[512,2048]{1,0:T(8,128)}) %all-reduce.5.cloned.1.call-update) | async-done | bytes 4194320 | tf_op jit(solution)/shard_map/psum | solution.py:17
  1239.2 11.1 collective-permute-done.23
  1375.7 11.6 convolution_subtract_fusion
  1409.2 42.8 %psum.23 = f32[2]{0:T(128)S(1)} all-reduce(f32[2]{0:T(128)S(1)} %pad_maximum_fusion.35), channel_id=1, replica_groups=mesh['row'=4,'col'=8] {'row','col'}, use_global_device_ids=true, to_apply=%region_66.68 | all-reduce | flops 2 | bytes 16 | tf_op jit(solution)/shard_map/psum | solution.py:130
  (819 shorter events, 744.8 us)
Async XLA Ops:
  7.2 113.6 %all-gather.9.cloned.1.call-start = ((), (), s32[]{:S(2)}) async-start(), calls=%async_computation.6 | async-start | bytes 2359296 | tf_op jit(solution)/shard_map/all_gather | solution.py:90
  93.3 163.2 %all-gather.11.cloned.1.call-start = ((), (), s32[]{:S(2)}) async-start(), calls=%async_computation.7 | async-start | bytes 2359296 | tf_op jit(solution)/shard_map/all_gather | solution.py:90
  122.8 14.1 collective-permute-start
  136.9 13.9 collective-permute-start.1
  150.9 14.5 collective-permute-start.2
  228.3 162.9 %all-gather.13.cloned.1.call-start = ((), (), s32[]{:S(2)}) async-start(), calls=%async_computation.8 | async-start | bytes 2359296 | tf_op jit(solution)/shard_map/all_gather | solution.py:90
  258.5 14.1 collective-permute-start.3
  272.6 13.8 collective-permute-start.4
  286.4 14.1 collective-permute-start.5
  363.0 162.4 %all-gather.15.cloned.1.call-start = ((), (), s32[]{:S(2)}) async-start(), calls=%async_computation.9 | async-start | bytes 2359296 | tf_op jit(solution)/shard_map/all_gather | solution.py:90
  393.2 14.1 collective-permute-start.6
  421.1 14.1 collective-permute-start.8
  497.3 162.8 %all-gather.17.cloned.1.call-start = ((), (), s32[]{:S(2)}) async-start(), calls=%async_computation.10 | async-start | bytes 2359296 | tf_op jit(solution)/shard_map/all_gather | solution.py:90
  527.5 14.1 collective-permute-start.9
  555.4 14.1 collective-permute-start.11
  632.0 162.4 %all-gather.19.cloned.1.call-start = ((), (), s32[]{:S(2)}) async-start(), calls=%async_computation.11 | async-start | bytes 2359296 | tf_op jit(solution)/shard_map/all_gather | solution.py:90
  662.1 14.1 collective-permute-start.12
  690.1 14.1 collective-permute-start.14
  766.2 162.8 %all-gather.21.cloned.1.call-start = ((), (), s32[]{:S(2)}) async-start(), calls=%async_computation.12 | async-start | bytes 2359296 | tf_op jit(solution)/shard_map/all_gather | solution.py:90
  796.4 14.1 collective-permute-start.15
  824.3 14.1 collective-permute-start.17
  900.9 112.9 %all-reduce.3.cloned.1.call-start = ((), (), s32[]{:S(2)}) async-start(), calls=%async_computation.4 | async-start | bytes 8388608 | tf_op jit(solution)/shard_map/psum | solution.py:17
  905.7 266.9 %all-reduce.5.cloned.1.call-start = ((), (), s32[]{:S(2)}) async-start(), calls=%async_computation.5 | async-start | bytes 8388608 | tf_op jit(solution)/shard_map/psum | solution.py:17
  931.1 14.1 collective-permute-start.18
  945.2 13.9 collective-permute-start.19
  959.1 60.2 %collective-permute-start.20 = (f32[128,1024]{1,0:T(8,128)}, f32[128,1024]{1,0:T(8,128)}, u32[]{:S(2)}, u32[]{:S(2)}) collective-permute-start(f32[128,1024]{1,0:T(8,128)} %collective-permute-done.19), channel_id=1, source_target_pairs={{0,8},{8,16},{16,24},{24,0},{1,9},{9,17},{17,25},{25,1},{2,10},{10... | collective-permute-start | bytes 1572872 | tf_op jit(solution)/shard_map/ppermute | solution.py:99
  1019.3 183.7 %all-gather.23.cloned.1.call-start = ((), (), s32[]{:S(2)}) async-start(), calls=%async_computation.13 | async-start | bytes 2359296 | tf_op jit(solution)/shard_map/all_gather | solution.py:90
  1207.8 14.4 collective-permute-start.21
  1222.2 14.0 collective-permute-start.22
  1236.2 14.1 collective-permute-start.23
  1311.0 50.2 %all-to-all-start.2 = ((f32[8,1,128,512]{3,2,1,0:T(8,128)}), f32[8,1,128,512]{3,2,1,0:T(8,128)}, u32[]{:S(2)}, u32[]{:S(2)}) async-start(f32[8,1,128,512]{3,2,1,0:T(8,128)} %bitcast.706), calls=%async_computation.2 | async-start | bytes 4194304 | tf_op jit(solution)/shard_map/all_to_all | solution.py:115
  1364.9 30.4 %all-to-all-start.3 = ((f32[8,1,64,1024]{3,2,1,0:T(8,128)}), f32[8,1,64,1024]{3,2,1,0:T(8,128)}, u32[]{:S(2)}, u32[]{:S(2)}) async-start(f32[8,1,64,1024]{3,2,1,0:T(8,128)} %bitcast.72), calls=%async_computation.3 | async-start | bytes 4194304 | tf_op jit(solution)/shard_map/all_to_all | solution.py:117
  (134 other events, 781.6 us)
Sparse Core Ops, SparseCore 0:
  93.5 27.2 all-gather.8
  228.4 28.0 all-gather.10
  363.2 27.9 all-gather.12
  497.5 27.9 all-gather.14
  632.1 27.9 all-gather.16
  766.4 27.9 all-gather.18
  901.0 27.9 all-gather.20
  932.9 80.8 all-reduce.2
  1019.4 153.0 all-reduce.4
  1174.3 28.6 all-gather.22
